TPU v7x, 1024 devices: a whole 4x4x32 slice. The times are simulated.
1024 devices in a mesh: fsdp: 64 (over x_hi, z), dp: 16 (over x_lo, y, core).
Axes of the slice: x: 4 (x_hi: 2, x_lo: 2; x = x_hi * 2 + x_lo), y: 4, z: 32, core: 2. Of those that a mesh axis runs over, the one named last changes fastest.
Arguments:
- qkv: bfloat16 [262144, 768], P(('fsdp', 'dp')), may hold values from -6 to 6
- segment: int32 [1024, 256], P(('fsdp', 'dp')), may hold values from 0 to 3, as said below
- handoff: int32 [1024], P(('fsdp', 'dp')), may hold values from 0 to 3, as said below
- qk_gain: float32 [2, 256], replicated, may hold values from 0.6 to 6
- d_head: bfloat16 [262144, 256], P(('fsdp', 'dp')), may hold values from -12 to 12
Outputs:
- grad_qkv: bfloat16 [262144, 768], P(('fsdp', 'dp'))
- attended: bfloat16 [262144, 256], P(('fsdp', 'dp'))
- handed: bfloat16 [1024, 160, 256], P(('fsdp', 'dp'))
- grad_gain: float32 [2, 256], replicated
Inputs may be any that keep to these rules, and one draw needn't show every extreme that they name: `segment`: image ids never fall along a pack; each of the 4 images of a pack has 1 to 160 patches, and one image of every pack has exactly 160. `handoff`: names an image of its own pack.
All inputs are finite; a program needn't handle non-finite values.
Results may differ from a plain program's by a relative error of at most 0.006.
The roundings to bfloat16 on the way count: a program that leaves them out, or rounds other values in their place, can miss the bound.
Values may be sent and summed in bfloat16 or wider, within the bound.
A program may use at most 32 MiB of HBM per device.

v0:
```python
import jax
import jax.numpy as jnp
from jax import lax
from jax.sharding import Mesh
from jax.sharding import PartitionSpec as P

HEAD = 128
MOST = 160
DP = ("dp_0", "dp_1", "dp_2")
FSDP_DP = ("fsdp_0", "fsdp_1", "dp_0", "dp_1", "dp_2")


epsilon = 1e-06


def swapped(value, axis, bit):
    mask = 2**bit
    pairs = [(source, source ^ mask) for source in range(lax.axis_size(axis))]
    return lax.ppermute(value, axis, pairs)


def by_axis(array, axes):
    for axis in axes:
        array = lax.psum(array, axis)
    return array


def head_norm(values, gain_vec):
    centre = jnp.mean(values, axis=-1, keepdims=True)
    shifted = values - centre
    spread = jnp.mean(shifted * shifted, axis=-1, keepdims=True)
    inverse = lax.rsqrt(spread + epsilon)
    centred = shifted * inverse
    return (centred * gain_vec, centred, inverse)


def norm_back(grad_out, centred, inverse, gain_vec):
    scaled = grad_out * gain_vec
    mean_first = jnp.mean(scaled, axis=-1, keepdims=True)
    mean_second = jnp.mean(scaled * centred, axis=-1, keepdims=True)
    return inverse * (scaled - mean_first - centred * mean_second)


def attend_heads(qkv_rows, allowed, cotangent, qk_gain):
    head_width = cotangent.shape[1]
    head_count = head_width // HEAD
    scaling = 1.0 / jnp.sqrt(jnp.float32(HEAD))
    outputs = []
    query_grads = []
    key_grads = []
    value_grads = []
    query_terms = []
    key_terms = []
    for head_index in range(head_count):
        col_low = head_index * HEAD
        col_high = col_low + HEAD
        query_part = qkv_rows[:, col_low:col_high].astype(jnp.float32)
        key_part = qkv_rows[:, head_width + col_low : head_width + col_high].astype(jnp.float32)
        value_low = qkv_rows[:, 2 * head_width + col_low : 2 * head_width + col_high]
        d_rows = cotangent[:, col_low:col_high]
        gain_query = qk_gain[0, col_low:col_high]
        gain_keys = qk_gain[1, col_low:col_high]
        query_n, query_hat, query_inv = head_norm(query_part, gain_query)
        keys_n, keys_hat, keys_inv = head_norm(key_part, gain_keys)
        query_low = query_n.astype(jnp.bfloat16)
        keys_low = keys_n.astype(jnp.bfloat16)
        scores = jnp.dot(query_low, keys_low.T, preferred_element_type=jnp.float32) * scaling
        scores = jnp.where(allowed, scores, jnp.float32(-1e30))
        scores = scores - jnp.max(scores, axis=-1, keepdims=True)
        exp_scores = jnp.where(allowed, jnp.exp(scores), jnp.float32(0.0))
        attend = exp_scores / jnp.sum(exp_scores, axis=-1, keepdims=True)
        attend_low = attend.astype(jnp.bfloat16)
        outputs.append(
            jnp.dot(attend_low, value_low, preferred_element_type=jnp.float32).astype(jnp.bfloat16)
        )
        grad_attend = jnp.dot(d_rows, value_low.T, preferred_element_type=jnp.float32)
        inner_sum = jnp.sum(grad_attend * attend, axis=-1, keepdims=True)
        grad_scores = (attend * (grad_attend - inner_sum) * scaling).astype(jnp.bfloat16)
        grad_query = jnp.dot(grad_scores, keys_low, preferred_element_type=jnp.float32)
        grad_keys = jnp.dot(grad_scores.T, query_low, preferred_element_type=jnp.float32)
        grad_value = jnp.dot(attend_low.T, d_rows, preferred_element_type=jnp.float32)
        query_terms.append(jnp.sum(grad_query * query_hat, axis=0))
        key_terms.append(jnp.sum(grad_keys * keys_hat, axis=0))
        query_grads.append(norm_back(grad_query, query_hat, query_inv, gain_query))
        key_grads.append(norm_back(grad_keys, keys_hat, keys_inv, gain_keys))
        value_grads.append(grad_value)
    output = jnp.concatenate(outputs, axis=1)
    grads = jnp.concatenate(query_grads + key_grads + value_grads, axis=1).astype(jnp.bfloat16)
    gain_terms = jnp.stack([jnp.concatenate(query_terms), jnp.concatenate(key_terms)])
    return (output, grads, gain_terms)


def take_rows(block, first_row, in_image):
    padded = jnp.concatenate([block, jnp.zeros((MOST, block.shape[1]), block.dtype)], axis=0)
    window = lax.dynamic_slice_in_dim(padded, first_row, MOST, 0)
    return jnp.where(in_image[:, None], window, jnp.zeros_like(window))


def body(qkv, segment, handoff, qk_gain, d_head):
    seg_row = segment[0]
    chosen = handoff[0]
    first_row = jnp.sum((seg_row < chosen).astype(jnp.int32))
    image_len = jnp.sum((seg_row == chosen).astype(jnp.int32))
    handed_rows = seg_row == chosen
    slot_index = jnp.arange(MOST, dtype=jnp.int32)
    in_image = slot_index < image_len
    allowed = seg_row[:, None] == seg_row[None, :]
    output, grad_qkv, gain_terms = attend_heads(qkv, allowed, d_head, qk_gain)
    out_piece = take_rows(output, first_row, in_image)
    handed = swapped(out_piece, DP, 0)
    attended = jnp.where(handed_rows[:, None], jnp.zeros_like(output), output)
    grad_gain = by_axis(gain_terms, FSDP_DP)
    return (grad_qkv, attended, handed[None], grad_gain)


def solution(mesh):
    split = Mesh(mesh.devices.reshape(2, 32, 2, 4, 2), ("fsdp_0", "fsdp_1", "dp_0", "dp_1", "dp_2"))
    placed = (P(FSDP_DP, None), P(FSDP_DP, None), P(FSDP_DP), P(), P(FSDP_DP, None))
    return jax.shard_map(
        body,
        mesh=split,
        in_specs=placed,
        out_specs=(P(FSDP_DP, None), P(FSDP_DP, None), P(FSDP_DP, None, None), P()),
        check_vma=False,
    )
```

profile of v0, /device:TPU:1, one launch (start us, length us, event | category | flops | bytes accessed | tf_op | source)
XLA Modules:
  0.0 113.4 jit_solution(14366901099941518975)
XLA Ops:
  0.6 1.0 fusion.96
  1.6 0.1 copy.16
  1.7 0.1 copy.17
  2.0 0.0 copy-start.2
  2.0 0.6 copy-done.2
  2.7 0.1 copy.19
  2.9 0.1 copy.18
  3.1 0.0 copy-start.1
  3.1 0.7 copy-done.1
  3.8 0.0 copy-start
  3.8 0.3 fusion.97
  4.1 0.1 fusion.7
  4.2 0.5 copy-done
  4.7 0.3 convolution_convert_fusion
  5.0 0.0 copy-start.3
  5.0 0.3 fusion.98
  5.4 0.6 copy-done.3
  5.9 0.2 multiply_reduce_fusion
  6.2 0.3 convolution_convert_fusion.1
  7.1 0.6 convert_reduce_fusion.4
  9.0 0.7 iota_compare_fusion
  10.4 0.1 fusion.60
  10.5 16.0 %collective-permute-start = (bf16[160,256]{0,1:T(8,128)(2,1)S(1)}, bf16[160,256]{0,1:T(8,128)(2,1)S(1)}, u32[]{:S(2)}, u32[]{:S(2)}) collective-permute-start(bf16[160,256]{0,1:T(8,128)(2,1)S(1)} %fusion.60), channel_id=1, source_target_pairs={{0,1},{1,0},{2,3},{3,2},{4,5},{5,4},{6,7},{7,6},{8,9},{9,8},{10,11... | collective-permute-start | bytes 245768 | tf_op jit(solution)/shard_map/ppermute | solution.py:19
  26.5 0.2 multiply_reduce_fusion.1
  26.7 0.2 multiply_convert_fusion
  27.0 0.3 fusion.58
  27.3 0.3 fusion.51
  27.6 0.3 fusion.44
  27.9 0.3 fusion.37
  28.3 0.1 fusion.61
  28.4 0.1 fusion.63
  28.5 0.1 fusion.62
  28.6 0.1 fusion.64
  28.7 0.3 fusion.3
  29.0 0.3 fusion.2
  29.3 0.9 copy.13
  30.2 0.8 copy.14
  31.0 5.3 %psum.35 = f32[2,256]{1,0:T(2,128)S(1)} all-reduce(f32[2,256]{1,0:T(2,128)S(1)} %pad_maximum_fusion.1), channel_id=1, replica_groups=mesh['fsdp_0'=2,'fsdp_1'=32,'dp_0'=2,'dp_1'=4,'dp_2'=2] {'fsdp_0'}, use_global_device_ids=true, to_apply=%region_28.29 | all-reduce | flops 512 | bytes 4096 | tf_op jit(solution)/shard_map/psum | solution.py:24
  36.3 42.7 %psum.36 = f32[2,256]{1,0:T(2,128)S(1)} all-reduce(f32[2,256]{1,0:T(2,128)S(1)} %psum.35), channel_id=1, replica_groups=mesh['fsdp_0'=2,'fsdp_1'=32,'dp_0'=2,'dp_1'=4,'dp_2'=2] {'fsdp_1'}, use_global_device_ids=true, to_apply=%region_29.30 | all-reduce | flops 512 | bytes 4096 | tf_op jit(solution)/shard_map/psum | solution.py:24
  78.9 4.1 %psum.37 = f32[2,256]{1,0:T(2,128)S(1)} all-reduce(f32[2,256]{1,0:T(2,128)S(1)} %psum.36), channel_id=1, replica_groups=mesh['fsdp_0'=2,'fsdp_1'=32,'dp_0'=2,'dp_1'=4,'dp_2'=2] {'dp_0'}, use_global_device_ids=true, to_apply=%region_30.31 | all-reduce | flops 512 | bytes 4096 | tf_op jit(solution)/shard_map/psum | solution.py:24
  83.0 8.7 %psum.38 = f32[2,256]{1,0:T(2,128)S(1)} all-reduce(f32[2,256]{1,0:T(2,128)S(1)} %psum.37), channel_id=1, replica_groups=mesh['fsdp_0'=2,'fsdp_1'=32,'dp_0'=2,'dp_1'=4,'dp_2'=2] {'dp_1'}, use_global_device_ids=true, to_apply=%region_31.32 | all-reduce | flops 512 | bytes 4096 | tf_op jit(solution)/shard_map/psum | solution.py:24
  91.7 20.9 %psum.39 = f32[2,256]{1,0:T(2,128)} all-reduce(f32[2,256]{1,0:T(2,128)S(1)} %psum.38), channel_id=1, replica_groups=mesh['fsdp_0'=2,'fsdp_1'=32,'dp_0'=2,'dp_1'=4,'dp_2'=2] {'dp_2'}, use_global_device_ids=true, to_apply=%region_32.33 | all-reduce | flops 512 | bytes 4096 | tf_op jit(solution)/shard_map/psum | solution.py:24
  112.6 0.0 collective-permute-done
  112.6 0.7 copy.15
  (27 shorter events, 0.4 us)
Async XLA Ops:
  2.0 0.7 copy-start.2
  3.1 0.7 copy-start.1
  3.8 1.0 copy-start
  5.0 0.9 copy-start.3
  10.5 102.1 %collective-permute-start = (bf16[160,256]{0,1:T(8,128)(2,1)S(1)}, bf16[160,256]{0,1:T(8,128)(2,1)S(1)}, u32[]{:S(2)}, u32[]{:S(2)}) collective-permute-start(bf16[160,256]{0,1:T(8,128)(2,1)S(1)} %fusion.60), channel_id=1, source_target_pairs={{0,1},{1,0},{2,3},{3,2},{4,5},{5,4},{6,7},{7,6},{8,9},{9,8},{10,11... | collective-permute-start | bytes 245768 | tf_op jit(solution)/shard_map/ppermute | solution.py:19
where the time goes:
time: 114 us; the launch traced here: 113 us
  blocking collectives  81.6 us (72%)
  starting transfers between devices  16 us (14%)
  local copies, waits for them, and re-layouts  6.25 us (5%)
  between operations  3.48 us (3%)
  matrix products  3.43 us (3%)
  other arithmetic  2.54 us (2%)
    psum x5, blocking collectives, by_axis(): array = lax.psum(array, axis)  81.6 us
    ppermute x1, starting transfers between devices, swapped(): return lax.ppermute(value, axis, pairs)  16 us
    unnamed x15, local copies, waits for them, and re-layouts  5.28 us
  transfers between devices with their start and end apart: 1, of which 0 were waited for; matrix products, arithmetic and copies ran while one was open for 4% of the time, Pallas kernels for 0%

commit v1 on v0

v1 whole, which is shorter than its diff:
```python
import jax
import jax.numpy as jnp
from jax import lax
from jax.experimental import pallas as pl
from jax.experimental.pallas import tpu as pltpu
from jax.sharding import Mesh
from jax.sharding import PartitionSpec as P

HEAD = 128
HEADS = 2
ROWS = 256
WIDTH = HEADS * HEAD
MOST = 160
IMAGES = 4
EPSILON = 1e-06
SCALE = 1.0 / HEAD**0.5

AXES = ("fsdp_0", "fsdp_1", "dp_0", "dp_1", "dp_2")
PLANES = 32
PLANE = 32
QUAD = 4
GROUPS = PLANES // QUAD
NEAR = sorted(((i, j) for i in range(4) for j in range(4)), key=lambda o: -(min(o[0], 4 - o[0]) + min(o[1], 4 - o[1])))
LOGICAL = pl.DeviceIdType.LOGICAL
F32 = jnp.float32
BF16 = jnp.bfloat16


def dot(a, b, a_dim, b_dim):
    return lax.dot_general(a, b, (((a_dim,), (b_dim,)), ((), ())), preferred_element_type=F32)


def head_norm(values, gain):
    shifted = values - jnp.mean(values, axis=-1, keepdims=True)
    inverse = lax.rsqrt(jnp.mean(shifted * shifted, axis=-1, keepdims=True) + EPSILON)
    hat = shifted * inverse
    return (hat * gain).astype(BF16), hat, inverse


def norm_back(grad, hat, inverse, gain):
    scaled = grad * gain
    first = jnp.mean(scaled, axis=-1, keepdims=True)
    second = jnp.mean(scaled * hat, axis=-1, keepdims=True)
    return inverse * (scaled - first - hat * second)


def kernel(
    qkv, seg, hand, gain, d_head,
    grad_out, attended_out, handed_out, sum_out,
    qkv_v, seg_v, hand_s, gain_v, d_v, taken_v, plane_v, quad_v, ring_v,
    load_sem, plane_send, plane_recv, quad_send, quad_recv, ring_send, ring_recv, hand_sem,
):
    x_hi, z, x_lo, y, core = (lax.axis_index(a) for a in AXES)
    low = x_lo * 8 + y * 2 + core
    mine = x_hi * 16 + low
    quad_at = lax.rem(z, QUAD)
    group_at = lax.div(z, QUAD)

    x = 2 * x_hi + x_lo
    xs = [lax.rem(x + k, 4) for k in range(4)]
    ys = [lax.rem(y + k, 4) for k in range(4)]
    cores = [core, 1 - core]
    slot_x = [8 * k for k in xs]
    device_x = [lax.div(k, 2) * 512 + lax.rem(k, 2) * 8 + z * 16 for k in xs]
    slot_y = [[2 * k + c for c in cores] for k in ys]
    plane = [
        (slot_x[i] + slot_y[j][c], device_x[i] + slot_y[j][c])
        for i, j in NEAR for c in range(2) if (i, j, c) != (0, 0, 0)
    ]

    def z_device(other):
        return x_hi * 512 + other * 16 + low

    partner = x_hi * 512 + z * 16 + low + 1 - 2 * core
    quad_at_of = [lax.rem(quad_at + k, QUAD) for k in range(QUAD)]
    quads = [group_at * QUAD + quad_at_of[k] for k in range(QUAD)]

    def at_offset(offset):
        return lax.rem(z + (offset + PLANES), PLANES)

    loads = [
        pltpu.make_async_copy(a, b, load_sem.at[i])
        for i, (a, b) in enumerate(((qkv, qkv_v), (seg, seg_v), (gain, gain_v), (d_head, d_v), (hand, hand_s)))
    ]
    for load in loads:
        load.start()
    barrier = pltpu.get_barrier_semaphore()

    for _, device in plane:
        pl.semaphore_signal(barrier, inc=1, device_id=device, device_id_type=LOGICAL)
    far = [quads[k] for k in range(1, QUAD)] + [at_offset(o) for o in (4, -4, 8, -8)]
    for other in far:
        pl.semaphore_signal(barrier, inc=1, device_id=z_device(other), device_id_type=LOGICAL)
    for load in loads:
        load.wait()

    seg_row = seg_v[...].astype(F32)
    row_id = lax.broadcasted_iota(jnp.int32, (ROWS, 1), 0).astype(F32)
    seg_col = jnp.zeros((ROWS, 1), F32)
    for image in range(1, IMAGES):
        end = jnp.sum(jnp.where(seg_row < image, 1.0, 0.0), axis=1, keepdims=True)
        seg_col = seg_col + jnp.where(row_id >= end, 1.0, 0.0)
    allowed = seg_col == seg_row
    gains = gain_v[...]
    kept = []
    terms = [[], []]
    for head in range(HEADS):
        cols = pl.ds(head * HEAD, HEAD)
        gain_q = gains[0:1, head * HEAD:(head + 1) * HEAD]
        gain_k = gains[1:2, head * HEAD:(head + 1) * HEAD]
        query_b, query_hat, query_inv = head_norm(qkv_v[:, cols].astype(F32), gain_q)
        keys_b, keys_hat, keys_inv = head_norm(qkv_v[:, pl.ds(WIDTH + head * HEAD, HEAD)].astype(F32), gain_k)
        value_b = qkv_v[:, pl.ds(2 * WIDTH + head * HEAD, HEAD)]
        d_b = d_v[:, cols]
        scores = jnp.where(allowed, dot(query_b, keys_b, 1, 1) * SCALE, -1e30)
        scores = scores - jnp.max(scores, axis=-1, keepdims=True)
        exps = jnp.where(allowed, jnp.exp(scores), 0.0)
        attend = exps / jnp.sum(exps, axis=-1, keepdims=True)
        grad_attend = dot(d_b, value_b, 1, 1)
        inner = jnp.sum(grad_attend * attend, axis=-1, keepdims=True)
        grad_scores = (attend * (grad_attend - inner) * SCALE).astype(BF16)
        grad_query = dot(grad_scores, keys_b, 1, 0)
        grad_keys = dot(grad_scores, query_b, 0, 0)
        terms[0].append(jnp.sum(grad_query * query_hat, axis=0, keepdims=True))
        terms[1].append(jnp.sum(grad_keys * keys_hat, axis=0, keepdims=True))
        kept.append((attend.astype(BF16), value_b, d_b, grad_query, query_hat, query_inv, gain_q,
                     grad_keys, keys_hat, keys_inv, gain_k))
    plane_v[mine] = jnp.concatenate(terms[0] + terms[1], axis=0)

    pl.semaphore_wait(barrier, PLANE - 1 + len(far))

    plane_sends = [
        pltpu.make_async_remote_copy(
            src_ref=plane_v.at[mine], dst_ref=plane_v.at[mine], send_sem=plane_send.at[i],
            recv_sem=plane_recv.at[mine], device_id=device, device_id_type=LOGICAL)
        for i, (_, device) in enumerate(plane)
    ]
    for copy in plane_sends:
        copy.start()

    chosen = hand_s[0].astype(F32)
    is_chosen = seg_row == chosen
    first = jnp.sum(jnp.where(seg_row < chosen, 1.0, 0.0), axis=1, keepdims=True)
    col_id = lax.broadcasted_iota(jnp.int32, (MOST, ROWS), 1).astype(F32)
    slot_id = lax.broadcasted_iota(jnp.int32, (MOST, ROWS), 0).astype(F32)
    take = jnp.where(jnp.logical_and(col_id - slot_id == first, is_chosen), 1.0, 0.0).astype(BF16)
    stays = seg_col != chosen
    for head in range(HEADS):
        cols = pl.ds(head * HEAD, HEAD)
        attend_b, value_b = kept[head][:2]
        output = dot(attend_b, value_b, 1, 0).astype(BF16)
        taken_v[:, cols] = dot(take, output, 1, 0).astype(BF16)
        attended_out[:, cols] = jnp.where(stays, output.astype(F32), 0.0).astype(BF16)
    hand_copy = pltpu.make_async_remote_copy(
        src_ref=taken_v, dst_ref=handed_out, send_sem=hand_sem.at[0], recv_sem=hand_sem.at[1],
        device_id=partner, device_id_type=LOGICAL)
    hand_copy.start()
    for head in range(HEADS):
        (attend_b, value_b, d_b, grad_query, query_hat, query_inv, gain_q,
         grad_keys, keys_hat, keys_inv, gain_k) = kept[head]
        grad_out[:, pl.ds(head * HEAD, HEAD)] = norm_back(grad_query, query_hat, query_inv, gain_q).astype(BF16)
        grad_out[:, pl.ds(WIDTH + head * HEAD, HEAD)] = norm_back(grad_keys, keys_hat, keys_inv, gain_k).astype(BF16)
        grad_out[:, pl.ds(2 * WIDTH + head * HEAD, HEAD)] = dot(attend_b, d_b, 0, 0).astype(BF16)

    for i, (slot, device) in enumerate(plane):
        pltpu.make_async_remote_copy(
            src_ref=plane_v.at[mine], dst_ref=plane_v.at[slot], send_sem=plane_send.at[i],
            recv_sem=plane_recv.at[slot], device_id=device, device_id_type=LOGICAL).wait_recv()
    quad_v[quad_at] = jnp.sum(plane_v[:PLANE], axis=0)

    def z_copy(buf, slot, send, recv, other):
        return pltpu.make_async_remote_copy(
            src_ref=buf.at[slot], dst_ref=buf.at[slot], send_sem=send, recv_sem=recv.at[slot],
            device_id=z_device(other), device_id_type=LOGICAL)

    sends = [z_copy(quad_v, quad_at, quad_send.at[k], quad_recv, quads[k]) for k in range(1, QUAD)]
    for copy in sends:
        copy.start()
    for k in range(1, QUAD):
        z_copy(quad_v, quad_at_of[k], quad_send.at[k], quad_recv, quads[k]).wait_recv()
    ring_v[group_at] = jnp.sum(quad_v[:QUAD], axis=0)

    def slot_at(offset):
        return lax.rem(group_at + (offset + GROUPS), GROUPS)

    ring = []
    for i, offset in enumerate((8, -8, 4, -4)):
        ring.append(z_copy(ring_v, group_at, ring_send.at[i], ring_recv, at_offset(offset)))
        ring[-1].start()
    for i, (heard, target) in enumerate(((1, -8), (-1, 8), (2, -8))):
        slot = slot_at(heard)
        forward = z_copy(ring_v, slot, ring_send.at[4 + i], ring_recv, at_offset(target))
        forward.wait_recv()
        forward.start()
        ring.append(forward)
    for heard in (-2, 3, -3, 4):
        z_copy(ring_v, slot_at(heard), ring_send.at[0], ring_recv, at_offset(8)).wait_recv()
    total = jnp.sum(ring_v[:GROUPS], axis=0)
    sum_out[...] = jnp.concatenate(
        [jnp.concatenate([total[2 * i:2 * i + 1], total[2 * i + 1:2 * i + 2]], axis=1) for i in range(2)], axis=0)

    for copy in plane_sends + sends + ring:
        copy.wait_send()
    hand_copy.wait()


def write_kernel(grad, attended, handed, total, grad_out, attended_out, handed_out, sum_out, sem):
    copies = [
        pltpu.make_async_copy(a, b, sem.at[i])
        for i, (a, b) in enumerate(
            ((grad, grad_out), (attended, attended_out), (handed, handed_out.at[0]), (total, sum_out)))
    ]
    for copy in copies:
        copy.start()
    for copy in copies:
        copy.wait()


def body(qkv, segment, handoff, qk_gain, d_head):
    anywhere = pl.BlockSpec(memory_space=pl.ANY)
    hbm = pl.BlockSpec(memory_space=pltpu.HBM)
    vmem = pl.BlockSpec(memory_space=pltpu.VMEM)
    dma = pltpu.SemaphoreType.DMA
    held = (
        pltpu.VMEM((ROWS, 3 * WIDTH), BF16), pltpu.VMEM((ROWS, WIDTH), BF16),
        pltpu.VMEM((MOST, WIDTH), BF16), pltpu.VMEM((2, WIDTH), F32),
    )
    results = pl.pallas_call(
        kernel,
        out_shape=held,
        in_specs=[hbm] * 5,
        out_specs=(vmem,) * 4,
        scratch_shapes=[
            pltpu.VMEM((ROWS, 3 * WIDTH), BF16), pltpu.VMEM((1, ROWS), jnp.int32), pltpu.SMEM((1,), jnp.int32),
            pltpu.VMEM((2, WIDTH), F32), pltpu.VMEM((ROWS, WIDTH), BF16), pltpu.VMEM((MOST, WIDTH), BF16),
            pltpu.VMEM((PLANE + 1, 4, HEAD), F32), pltpu.VMEM((QUAD + 1, 4, HEAD), F32), pltpu.VMEM((GROUPS + 1, 4, HEAD), F32),
            dma((5,)), dma((PLANE,)), dma((PLANE,)), dma((QUAD,)), dma((QUAD,)), dma((8,)), dma((GROUPS,)), dma((2,)),
        ],
        compiler_params=pltpu.CompilerParams(collective_id=0, has_side_effects=True),
        name="pack_backward",
    )(qkv, segment, handoff, qk_gain, d_head)
    return pl.pallas_call(
        write_kernel,
        out_shape=(
            jax.ShapeDtypeStruct((ROWS, 3 * WIDTH), BF16), jax.ShapeDtypeStruct((ROWS, WIDTH), BF16),
            jax.ShapeDtypeStruct((1, MOST, WIDTH), BF16), jax.ShapeDtypeStruct((2, WIDTH), F32),
        ),
        in_specs=[vmem] * 4,
        out_specs=(anywhere,) * 4,
        scratch_shapes=[dma((4,))],
        name="write_out",
    )(*(pltpu.with_memory_space_constraint(r, pltpu.VMEM) for r in results))


def solution(mesh):
    split = Mesh(mesh.devices.reshape(2, 32, 2, 4, 2), AXES)
    rows = P(AXES, None)
    return jax.shard_map(
        body,
        mesh=split,
        in_specs=(rows, rows, P(AXES), P(), rows),
        out_specs=(rows, rows, P(AXES, None, None), P()),
        check_vma=False,
    )
```

time: 114 us -> 49.2 us (0.43)
  blocking collectives: 81.6 us -> 0 us
  Pallas kernels: 0 us -> 47.2 us
  starting transfers between devices: 16 us -> 0 us
  local copies, waits for them, and re-layouts: 6.25 us -> 0 us
  matrix products: 3.43 us -> 0 us
  other arithmetic: 2.54 us -> 0 us
  between operations: 3.48 us -> 1.29 us
    psum x5 -> x0, blocking collectives: 81.6 us -> none  [by_axis(): array = lax.psum(array, axis)]
    pallas_call x0 -> x2, Pallas kernels: none -> 47.2 us  [the longest x1 46.3 us: body(): pl.pallas_call(kernel, out_shape=held, in_specs=[hbm] * 5, out_specs=(vme...]
    ppermute x1 -> x0, starting transfers between devices: 16 us -> none  [swapped(): return lax.ppermute(value, axis, pairs)]
    unnamed x15 -> x0, local copies, waits for them, and re-layouts: 5.28 us -> none
    dot_general x12 -> x0, matrix products: 3.43 us -> none  [the longest x2 0.65 us: attend_heads(): jnp.dot(query_low, keys_low.T, preferred_element_type=jnp.float32) * scaling]
  transfers between devices with their start and end apart: 1 -> 0, of which waited for: 0 -> 0; matrix products, arithmetic and copies ran while one was open for 4% -> 0% of each run, Pallas kernels for 0% -> 0%
where the time goes in v1:
time: 49.2 us; the launch traced here: 48.5 us
  Pallas kernels  47.2 us (96%)
  between operations  1.29 us (3%)
    pallas_call x1, Pallas kernels, body(): pl.pallas_call(kernel, out_shape=held, in_specs=[hbm] * 5, out_specs=(vme...  46.3 us

profile of v1, /device:TPU:1, one launch (start us, length us, event | category | flops | bytes accessed | tf_op | source)
XLA Modules:
  0.0 48.5 jit_solution(7600594955496529858)
XLA Ops:
  1.3 46.3 %pack_backward.1 = (bf16[256,768]{1,0:T(8,128)(2,1)S(1)}, bf16[256,256]{1,0:T(8,128)(2,1)S(1)}, bf16[160,256]{1,0:T(8,128)(2,1)S(1)}, f32[2,256]{1,0:T(2,128)S(1)}) custom-call(bf16[256,768]{1,0:T(8,128)(2,1)} %qkv.1, s32[1,256]{1,0:T(1,128)} %seg.1, s32[1]{0:T(128)S(6)} %copy.9.hand, f32[2,256]{1,0:T(2,128)} %gain.1, bf16[256,256]{1,0:T(8,128)(2,1)} %d_head.1), custom_call_target="tpu_custom_call" | custom-call | tf_op jit(solution)/shard_map/pack_backward/pallas_call | solution.py:228
  47.6 0.8 %write_out.1 = (bf16[256,768]{1,0:T(8,128)(2,1)}, bf16[256,256]{1,0:T(8,128)(2,1)}, bf16[1,160,256]{2,1,0:T(8,128)(2,1)}, f32[2,256]{1,0:T(2,128)}) custom-call(bf16[256,768]{1,0:T(8,128)(2,1)S(1)} %get-tuple-element.8.grad, bf16[256,256]{1,0:T(8,128)(2,1)S(1)} %get-tuple-element.9.attended, bf16[160,256]{1,0:T(8,128)(2,1)S(1)} %get-tuple-element.10.handed, ...), custom_call_target="tpu_custom_call" | custom-call | tf_op jit(solution)/shard_map/write_out/pallas_call | solution.py:242
